TPU v7x, 32 devices: a whole 2x2x4 slice. The times are simulated.
32 devices in a mesh: dp: 8 (over z, y), expert: 4 (over x, core).
Axes of the slice: x: 2, y: 2, z: 4, core: 2. Of those that a mesh axis runs over, the one named last changes fastest.
Arguments:
- queries: bfloat16 [4096, 4096], P('dp', 'expert'), may hold values from -6 to 6
- key_states: bfloat16 [4096, 4096], P('dp', 'expert'), may hold values from -6 to 6
- value_states: bfloat16 [4096, 4096], P('dp', 'expert'), may hold values from -6 to 6
- doc_lengths: int32 [8, 8], replicated, may hold values from 0 to 512, as said below
- move_plan: int32 [8, 2], replicated, may hold values from 0 to 7, as said below
- expert_ids: int32 [4096, 8], P('dp'), may hold values from 0 to 15, all different within a row; in each aligned block of 512 rows (0 to 511, 512 to 1023, ...) at most 384 rows name the same one
- gate_weights: float32 [4096, 8], P('dp'), may hold values from 0.05 to 0.5
- expert_weight: bfloat16 [16, 4096, 1024], P('expert'), may hold values from -0.29882812 to 0.29882812
Outputs:
- attended: bfloat16 [4096, 4096], P('dp', 'expert')
- combined: bfloat16 [4096, 1024], P('dp', 'expert')
- row_load: float32 [8], P('dp')
Inputs may be any that keep to these rules, and one draw needn't show every extreme that they name: `doc_lengths`: each row's entries are the lengths of its packed documents in order and sum to 512; a zero marks an absent document; some row holds a single document. move_plan[r, 0] is r itself or the row half the dp axis away, (r + 8 / 2) mod 8; a row is handed to its partner only if its pairs in all exceed the partner's, so two partners never both move; move_plan[r, 1] is a block number below 2; at least one row moves a block. `expert_ids`: each token names 8 different experts; among the 512 tokens of one row no expert is named by more than 384 tokens.
All inputs are finite; a program needn't handle non-finite values.
Results may differ from a plain program's by a relative error of at most 0.0095.
Values may be sent and summed in bfloat16 or wider, within the bound.
A program may use at most 128 MiB of HBM per device.

v0:
```python
import jax
import jax.numpy as jnp
from jax import lax
from jax.sharding import PartitionSpec as P

HEAD_DIM = 128
QBLOCK = 128
BLOCKS = 4
EXPERTS = 16
CAP = 384


def token_starts(row_lengths, row_count):
    bounds = jnp.cumsum(row_lengths)
    positions = jnp.arange(row_count, dtype=jnp.int32)
    return jnp.max(jnp.where(bounds[None, :] <= positions[:, None], bounds[None, :], 0), axis=1)


def block_pairs(row_lengths, row_count):
    positions = jnp.arange(row_count, dtype=jnp.int32)
    reach = positions - token_starts(row_lengths, row_count) + 1
    return reach.reshape(BLOCKS, QBLOCK).sum(axis=1)


def attend(query_rows, key_rows, value_rows, query_positions, query_starts):
    query_count = query_rows.shape[0]
    key_count = key_rows.shape[0]
    head_count = query_rows.shape[1] // HEAD_DIM
    query_heads = query_rows.reshape(query_count, head_count, HEAD_DIM)
    key_heads = key_rows.reshape(key_count, head_count, HEAD_DIM)
    value_heads = value_rows.reshape(key_count, head_count, HEAD_DIM)
    scores = jnp.einsum(
        "qhd,khd->hqk", query_heads, key_heads, preferred_element_type=jnp.float32
    ) * HEAD_DIM ** (-0.5)
    key_positions = jnp.arange(key_count, dtype=jnp.int32)
    allowed = (key_positions[None, :] <= query_positions[:, None]) & (
        key_positions[None, :] >= query_starts[:, None]
    )
    scores = jnp.where(allowed[None], scores, -jnp.inf)
    weights = jax.nn.softmax(scores, axis=-1).astype(jnp.bfloat16)
    output = jnp.einsum("hqk,khd->qhd", weights, value_heads, preferred_element_type=jnp.float32)
    return output.reshape(query_count, head_count * HEAD_DIM).astype(jnp.bfloat16)


def shards(
    queries,
    key_states,
    value_states,
    doc_lengths,
    move_plan,
    expert_ids,
    gate_weights,
    expert_weight,
):
    dp_size = lax.axis_size("dp")
    group_size = lax.axis_size("expert")
    own_row = lax.axis_index("dp")
    partner = (own_row + dp_size // 2) % dp_size
    row_count = queries.shape[0]
    positions = jnp.arange(row_count, dtype=jnp.int32)
    own_lengths = lax.dynamic_index_in_dim(doc_lengths, own_row, 0, keepdims=False)
    partner_lengths = lax.dynamic_index_in_dim(doc_lengths, partner, 0, keepdims=False)
    own_starts = token_starts(own_lengths, row_count)
    own_plan = lax.dynamic_index_in_dim(move_plan, own_row, 0, keepdims=False)
    partner_plan = lax.dynamic_index_in_dim(move_plan, partner, 0, keepdims=False)
    moving = own_plan[0] != own_row
    incoming = partner_plan[0] != partner
    own_block = own_plan[1]
    their_block = partner_plan[1]

    def run_block(block_index):
        low_row = block_index * QBLOCK
        high_row = low_row + QBLOCK
        return attend(
            queries[low_row:high_row],
            key_states[:high_row],
            value_states[:high_row],
            positions[low_row:high_row],
            own_starts[low_row:high_row],
        )

    attended = jnp.concatenate([run_block(block_index) for block_index in range(BLOCKS)], 0)
    own_pairs = block_pairs(own_lengths, row_count)
    partner_pairs = block_pairs(partner_lengths, row_count)
    row_work = (
        jnp.sum(own_pairs)
        - jnp.where(moving, own_pairs[own_block], 0)
        + jnp.where(incoming, partner_pairs[their_block], 0)
    )
    row_load = (row_work.astype(jnp.float32) / (QBLOCK * QBLOCK)).reshape(1)
    local_experts = EXPERTS // group_size
    expert_range = jnp.arange(EXPERTS, dtype=jnp.int32)
    matches = expert_ids[:, :, None] == expert_range[None, None, :]
    member = jnp.any(matches, axis=1)
    gate_table = jnp.sum(jnp.where(matches, gate_weights[:, :, None], 0.0), axis=1)
    earlier = (positions[None, :] < positions[:, None]).astype(jnp.bfloat16)
    slot_counts = jnp.dot(earlier, member.astype(jnp.bfloat16), preferred_element_type=jnp.float32)
    slot_of = slot_counts.astype(jnp.int32)
    slot_range = jnp.arange(CAP, dtype=jnp.int32)
    dispatch_hot = member.T[:, None, :] & (slot_of.T[:, None, :] == slot_range[None, :, None])
    filled = jnp.any(dispatch_hot, axis=2)
    source = jnp.sum(jnp.where(dispatch_hot, positions[None, None, :], 0), axis=2) + jnp.where(
        filled, 0, row_count
    )
    source = source.reshape(-1)
    member_index = lax.axis_index("expert")
    chosen_rows = lax.dynamic_slice_in_dim(
        source, member_index * local_experts * CAP, local_experts * CAP, 0
    )
    piece = lax.all_gather(attended, "expert", axis=1, tiled=True)
    extended = jnp.concatenate([piece, jnp.zeros((1, piece.shape[1]), piece.dtype)], 0)
    picked = extended[chosen_rows].reshape(local_experts, CAP, piece.shape[1])
    summed = jnp.einsum("ecf,efg->ecg", picked, expert_weight, preferred_element_type=jnp.float32)
    activated = jax.nn.silu(summed).astype(jnp.bfloat16)[None]
    spread = lax.all_to_all(activated, "expert", split_axis=3, concat_axis=0, tiled=True)
    outputs_table = spread.reshape(EXPERTS, CAP, spread.shape[3])
    selected = jnp.einsum(
        "ect,ecg->teg",
        dispatch_hot.astype(jnp.bfloat16),
        outputs_table,
        preferred_element_type=jnp.float32,
    )
    combined = jnp.sum(selected * gate_table[:, :, None], axis=1).astype(jnp.bfloat16)
    return (attended, combined, row_load)


def solution(mesh):
    in_specs = (
        P("dp", "expert"),
        P("dp", "expert"),
        P("dp", "expert"),
        P(),
        P(),
        P("dp", None),
        P("dp", None),
        P("expert", None, None),
    )
    out_specs = (P("dp", "expert"), P("dp", "expert"), P("dp"))
    return jax.shard_map(shards, mesh=mesh, in_specs=in_specs, out_specs=out_specs, check_vma=False)
```

profile of v0, /device:TPU:0, one launch (start us, length us, event | category | flops | bytes accessed | tf_op | source)
XLA Modules:
  0.0 178.1 jit_solution(11677466727423004778)
XLA Ops:
  7.2 0.8 fusion.53
  8.3 1.3 fusion.57
  10.3 1.6 multiply_select_fusion.2
  11.8 0.8 fusion.64
  13.5 0.6 fusion.65
  14.7 1.3 copy.115
  16.0 1.2 copy.95
  17.2 4.2 %convolution_convert_fusion.2 = bf16[8,128,128]{1,2,0:T(8,128)(2,1)S(1)} fusion(bf16[384,8,128]{0,2,1:T(8,128)(2,1)} %bitcast.113, f32[8,128]{1,0:T(8,128)S(1)} %fusion.64, f32[8,128,384]{2,1,0:T(8,128)} %multiply_select_fusion.2), kind=kOutput, calls=%fused_computation.34 | convolution fusion | flops 101975424 | bytes 2625536 | tf_op jit(solution)/shard_map/hqk,khd->qhd/dot_general | solution.py:41
  21.4 0.9 copy.102
  22.5 1.9 %convolution_convert_fusion.3 = bf16[8,128,128]{1,2,0:T(8,128)(2,1)S(1)} fusion(bf16[256,8,128]{0,2,1:T(8,128)(2,1)S(1)} %bitcast.114, f32[8,128]{1,0:T(8,128)S(1)} %fusion.65, f32[8,128,256]{2,1,0:T(8,128)S(1)} %fusion.19), kind=kOutput, calls=%fused_computation.35 | convolution fusion | flops 68027648 | bytes 1839104 | tf_op jit(solution)/shard_map/hqk,khd->qhd/dot_general | solution.py:41
  26.4 2.3 %fusion.61 = (f32[8,128]{1,0:T(8,128)S(1)}, f32[8,128,512]{2,1,0:T(8,128)}) fusion(pred[128,512]{1,0:T(8,128)(4,1)S(1)} %fusion.32, bf16[128,8,128]{0,2,1:T(8,128)(2,1)S(1)} %bitcast.115, bf16[512,1024]{1,0:T(8,128)(2,1)S(1)} %copy-done.1), kind=kOutput, calls=%fused_computation.98 | convolution fusion | flops 136315392 | bytes 3477504 | tf_op jit(solution)/shard_map/sub | solution.py:40
  28.7 2.2 %convolution_convert_fusion = bf16[8,128,128]{1,2,0:T(8,128)(2,1)S(1)} fusion(bf16[512,8,128]{0,2,1:T(8,128)(2,1)S(1)} %bitcast.108, f32[8,128,512]{2,1,0:T(8,128)} %get-tuple-element.26, f32[8,128]{1,0:T(8,128)S(1)} %get-tuple-element.25), kind=kOutput, calls=%fused_computation.32 | convolution fusion | flops 135397376 | bytes 3411968 | tf_op jit(solution)/shard_map/hqk,khd->qhd/dot_general | solution.py:41
  31.1 1.0 pad_maximum_fusion
  32.4 2.1 %fusion.7 = pred[16,384]{1,0:T(8,128)(4,1)S(1)} fusion(s32[16,512]{1,0:T(8,128)S(1)} %convolution_convert_fusion.4, pred[16,512]{1,0:T(8,128)(4,1)S(1)} %bitcast.121), kind=kLoop, calls=%fused_computation.9 | loop fusion | flops 9431040 | bytes 47104 | tf_op jit(solution)/shard_map/reduce_or | solution.py:101
  34.5 2.8 %select_reduce_fusion = s32[16,384]{1,0:T(8,128)S(1)} fusion(s32[16,512]{1,0:T(8,128)S(1)} %convolution_convert_fusion.4, pred[16,512]{1,0:T(8,128)(4,1)S(1)} %bitcast.122), kind=kLoop, calls=%fused_computation.5 | loop fusion | flops 12576768 | bytes 65536 | tf_op jit(solution)/shard_map/reduce_sum | solution.py:102
  37.4 32.1 %all-gather.2.cloned.1.call-done = bf16[512,4096]{1,0:T(8,128)(2,1)} async-done(((bf16[512,1024]{1,0:T(8,128)(2,1)}), bf16[512,4096]{1,0:T(8,128)(2,1)}) %all-gather.2.cloned.1.call-update) | async-done | bytes 4194320 | tf_op jit(solution)/shard_map/all_gather | solution.py:110
  69.5 4.7 %concatenate.7 = bf16[513,4096]{1,0:T(8,128)(2,1)} pad(bf16[512,4096]{1,0:T(8,128)(2,1)} %all-gather.2.cloned.1.call-done, bf16[]{:T(256)} %constant.66.clone.1), padding=0_1x0_0 | pad | bytes 8396802 | tf_op jit(solution)/shard_map/concatenate | solution.py:111
  74.2 25.0 %gather_fusion = bf16[1536,4096]{1,0:T(8,128)(2,1)} fusion(bf16[513,4096]{1,0:T(8,128)(2,1)} %concatenate.7, s32[2048]{0:T(1024)S(1)} %pad_clamp_fusion), kind=kCustom, calls=%fused_computation | custom fusion | bytes 25171968 | tf_op jit(solution)/shard_map/gather | solution.py:112
  99.2 21.3 %fusion.11 = bf16[1,4,384,1024]{3,2,1,0:T(8,128)(2,1)S(1)} fusion(bf16[4,384,4096]{2,1,0:T(8,128)(2,1)} %bitcast.99, bf16[4,4096,1024]{2,1,0:T(8,128)(2,1)} %param.15), kind=kOutput, calls=%fused_computation.15 | convolution fusion | flops 12892766208 | bytes 49283072 | tf_op jit(solution)/shard_map/ecf,efg->ecg/dot_general | solution.py:113
  120.5 3.8 %copy.104 = bf16[1,4,384,1024]{2,1,0,3:T(4,128)(2,1)} copy(bf16[1,4,384,1024]{3,2,1,0:T(8,128)(2,1)S(1)} %fusion.11) | data formatting | bytes 6291456 | tf_op jit(solution)/shard_map/broadcast_in_dim | solution.py:114
  124.3 4.1 %all-to-all-start = ((bf16[1,4,384,1024]{2,1,0,3:T(4,128)(2,1)}), bf16[1,4,384,1024]{2,1,0,3:T(4,128)(2,1)S(1)}, u32[]{:S(2)}, u32[]{:S(2)}) async-start(bf16[1,4,384,1024]{2,1,0,3:T(4,128)(2,1)} %copy.104), calls=%async_computation | async-start | bytes 6291456 | tf_op jit(solution)/shard_map/all_to_all | solution.py:115
  138.3 26.6 %all-to-all-done = bf16[1,4,384,1024]{2,1,0,3:T(4,128)(2,1)S(1)} async-done(((bf16[1,4,384,1024]{2,1,0,3:T(4,128)(2,1)}), bf16[1,4,384,1024]{2,1,0,3:T(4,128)(2,1)S(1)}, u32[]{:S(2)}, u32[]{:S(2)}) %all-to-all-start) | async-done | bytes 3145760 | tf_op jit(solution)/shard_map/all_to_all | solution.py:115
  165.5 3.8 %fusion.8 = bf16[512,256]{0,1:T(8,128)(2,1)S(1)} fusion(f32[512,16]{0,1:T(8,128)S(1)} %select_reduce_fusion.1, bf16[16,384,256]{1,2,0:T(8,128)(2,1)S(1)} %bitcast.101, s32[16,512]{1,0:T(8,128)S(1)} %convolution_convert_fusion.4, pred[16,512]{1,0:T(8,128)(4,1)S(1)} %bitcast.123), kind=kOutput, calls=%fused_computation.11 | convolution fusion | flops 1620967424 | bytes 3481600 | tf_op jit(solution)/shard_map/ect,ecg->teg/dot_general | solution.py:117
  169.3 0.8 copy.106
  (76 shorter events, 8.5 us)
Async XLA Ops:
  7.2 2.6 %slice-start.3 = ((bf16[512,1024]{1,0:T(8,128)(2,1)}), bf16[384,1024]{1,0:T(8,128)(2,1)S(1)}, s32[]{:S(2)}) async-start(bf16[512,1024]{1,0:T(8,128)(2,1)} %param.9), calls=%async_computation.5 | async-start | bytes 1572864 | tf_op jit(solution)/shard_map/slice | solution.py:76
  7.2 62.3 %all-gather.2.cloned.1.call-start = ((), (), s32[]{:S(2)}) async-start(), calls=%async_computation.1 | async-start | bytes 5242880 | tf_op jit(solution)/shard_map/all_gather | solution.py:110
  10.2 2.5 %slice-start.4 = ((bf16[512,1024]{1,0:T(8,128)(2,1)}), bf16[256,1024]{1,0:T(8,128)(2,1)S(1)}, s32[]{:S(2)}) async-start(bf16[512,1024]{1,0:T(8,128)(2,1)} %param.9), calls=%async_computation.6 | async-start | bytes 1048576 | tf_op jit(solution)/shard_map/slice | solution.py:76
  13.5 1.2 copy-start
  14.1 1.9 %slice-start = ((bf16[512,1024]{1,0:T(8,128)(2,1)}), bf16[384,1024]{1,0:T(8,128)(2,1)S(1)}, s32[]{:S(2)}) async-start(bf16[512,1024]{1,0:T(8,128)(2,1)} %param.10), calls=%async_computation.2 | async-start | bytes 1572864 | tf_op jit(solution)/shard_map/slice | solution.py:77
  17.2 5.0 %slice-start.1 = ((bf16[512,1024]{1,0:T(8,128)(2,1)}), bf16[256,1024]{1,0:T(8,128)(2,1)S(1)}, s32[]{:S(2)}) async-start(bf16[512,1024]{1,0:T(8,128)(2,1)} %param.10), calls=%async_computation.3 | async-start | bytes 1048576 | tf_op jit(solution)/shard_map/slice | solution.py:77
  22.4 2.3 %slice-start.5 = ((bf16[512,1024]{1,0:T(8,128)(2,1)}), bf16[128,1024]{1,0:T(8,128)(2,1)S(1)}, s32[]{:S(2)}) async-start(bf16[512,1024]{1,0:T(8,128)(2,1)} %param.9), calls=%async_computation.7 | async-start | bytes 524288 | tf_op jit(solution)/shard_map/slice | solution.py:76
  22.4 3.0 %slice-start.2 = ((bf16[512,1024]{1,0:T(8,128)(2,1)}), bf16[128,1024]{1,0:T(8,128)(2,1)S(1)}, s32[]{:S(2)}) async-start(bf16[512,1024]{1,0:T(8,128)(2,1)} %param.10), calls=%async_computation.4 | async-start | bytes 524288 | tf_op jit(solution)/shard_map/slice | solution.py:77
  24.8 1.6 copy-start.1
  25.9 2.8 %copy-start.2 = (bf16[512,1024]{0,1:T(8,128)(2,1)S(1)}, bf16[512,1024]{0,1:T(8,128)(2,1)}, u32[]{:S(2)}) copy-start(bf16[512,1024]{0,1:T(8,128)(2,1)} %copy.115) | copy-start | bytes 3145732
  28.7 2.3 %copy-start.3 = (bf16[128,1024]{1,0:T(8,128)(2,1)S(1)}, bf16[128,1024]{1,0:T(8,128)(2,1)}, u32[]{:S(2)}) copy-start(bf16[128,1024]{1,0:T(8,128)(2,1)} %copy.102) | copy-start | bytes 786436
  30.9 1.2 copy-start.4
  124.3 4.1 %copy-start.6 = (s32[8,2]{0,1:T(2,128)S(1)}, s32[8,2]{0,1:T(2,128)}, u32[]{:S(2)}) copy-start(s32[8,2]{0,1:T(2,128)} %param.12) | copy-start | bytes 196
  124.3 14.0 %copy-start.5 = (f32[512,8]{0,1:T(8,128)S(1)}, f32[512,8]{0,1:T(8,128)}, u32[]{:S(2)}) copy-start(f32[512,8]{0,1:T(8,128)} %param.14) | copy-start | bytes 49156
  124.3 40.7 %all-to-all-start = ((bf16[1,4,384,1024]{2,1,0,3:T(4,128)(2,1)}), bf16[1,4,384,1024]{2,1,0,3:T(4,128)(2,1)S(1)}, u32[]{:S(2)}, u32[]{:S(2)}) async-start(bf16[1,4,384,1024]{2,1,0,3:T(4,128)(2,1)} %copy.104), calls=%async_computation | async-start | bytes 6291456 | tf_op jit(solution)/shard_map/all_to_all | solution.py:115
Sparse Core Ops, SparseCore 0:
  32.2 37.1 all-gather.1
where the time goes:
time: 179 us; the launch traced here: 178 us
  waiting for transfers between devices  58.7 us (33%)
  local copies, waits for them, and re-layouts  44.9 us (25%)
  matrix products  39.8 us (22%)
  between operations  22.6 us (13%)
  other arithmetic  7.99 us (4%)
  starting transfers between devices  4.13 us (2%)
    all_gather x1, waiting for transfers between devices, shards(): piece = lax.all_gather(attended, 'expert', axis=1, tiled=True)  32.1 us
    all_to_all x1, waiting for transfers between devices, shards(): lax.all_to_all(activated, 'expert', split_axis=3, concat_axis=0, tiled=True)  26.6 us
    gather x1, local copies, waits for them, and re-layouts, shards(): picked = extended[chosen_rows].reshape(local_experts, CAP, piece.shape[1])  25 us
    dot_general x1, matrix products, shards(): jnp.einsum('ecf,efg->ecg', picked, expert_weight, preferred_element_type=...  21.3 us
    dot_general x4, matrix products, attend(): jnp.einsum('hqk,khd->qhd', weights, value_heads, preferred_element_type=j...  8.57 us
    concatenate x1, local copies, waits for them, and re-layouts, shards(): jnp.concatenate([piece, jnp.zeros((1, piece.shape[1]), piece.dtype)], 0)  4.7 us
    all_to_all x1, starting transfers between devices, shards(): lax.all_to_all(activated, 'expert', split_axis=3, concat_axis=0, tiled=True)  4.09 us
    broadcast_in_dim x1, local copies, waits for them, and re-layouts, shards(): activated = jax.nn.silu(summed).astype(jnp.bfloat16)[None]  3.76 us
  transfers between devices with their start and end apart: 2, of which 2 were waited for; matrix products, arithmetic and copies ran while one was open for 5% of the time, Pallas kernels for 0%

commit v1 on v0

--- a/solution.py
+++ b/solution.py
@@ -52,6 +52,19 @@
     gate_weights,
     expert_weight,
 ):
+
+    def points_scan(block_here, d0):
+        nodes = jax.lax.axis_size("expert")
+        buffer = []
+        for u in range(nodes):
+            buffer.append((u, (u + 1) % nodes))
+        back = [None] * nodes
+        back[nodes - 1] = block_here
+        for c in range(nodes - 2, -1, -1):
+            back[c] = jax.lax.ppermute(back[c + 1], axis_name="expert", perm=buffer)
+        y = jnp.concatenate(back, axis=d0)
+        return jnp.roll(y, (jax.lax.axis_index("expert") + 1) * block_here.shape[d0], axis=d0)
+
     dp_size = lax.axis_size("dp")
     group_size = lax.axis_size("expert")
     own_row = lax.axis_index("dp")
@@ -107,7 +120,7 @@
     chosen_rows = lax.dynamic_slice_in_dim(
         source, member_index * local_experts * CAP, local_experts * CAP, 0
     )
-    piece = lax.all_gather(attended, "expert", axis=1, tiled=True)
+    piece = points_scan(attended, d0=1)
     extended = jnp.concatenate([piece, jnp.zeros((1, piece.shape[1]), piece.dtype)], 0)
     picked = extended[chosen_rows].reshape(local_experts, CAP, piece.shape[1])
     summed = jnp.einsum("ecf,efg->ecg", picked, expert_weight, preferred_element_type=jnp.float32)

time: 179 us -> 172 us (0.961)
  between operations: 22.6 us -> 9.37 us
  waiting for transfers between devices: 58.7 us -> 63.8 us
    ppermute x0 -> x3, waiting for transfers between devices: none -> 37.1 us  [points_scan(): back[c] = jax.lax.ppermute(back[c + 1], axis_name='expert', perm=buffer)]
    all_gather x1 -> x0, waiting for transfers between devices: 32.1 us -> none  [shards(): piece = lax.all_gather(attended, 'expert', axis=1, tiled=True)]
    concatenate x1, local copies, waits for them, and re-layouts: 4.7 us -> 2.46 us  [shards(): jnp.concatenate([piece, jnp.zeros((1, piece.shape[1]), piece.dtype)], 0)]
    unnamed x22 -> x42, local copies, waits for them, and re-layouts: 2.83 us -> 4.49 us
  transfers between devices with their start and end apart: 2 -> 4, of which waited for: 2 -> 4; matrix products, arithmetic and copies ran while one was open for 5% -> 5% of each run, Pallas kernels for 0% -> 0%
where the time goes in v1:
time: 172 us; the launch traced here: 171 us
  waiting for transfers between devices  63.8 us (37%)
  local copies, waits for them, and re-layouts  45.7 us (27%)
  matrix products  40.5 us (24%)
  between operations  9.37 us (5%)
  other arithmetic  7.13 us (4%)
  starting transfers between devices  4.64 us (3%)
    ppermute x3, waiting for transfers between devices, points_scan(): back[c] = jax.lax.ppermute(back[c + 1], axis_name='expert', perm=buffer)  37.1 us
    all_to_all x1, waiting for transfers between devices, shards(): lax.all_to_all(activated, 'expert', split_axis=3, concat_axis=0, tiled=True)  26.6 us
    gather x1, local copies, waits for them, and re-layouts, shards(): picked = extended[chosen_rows].reshape(local_experts, CAP, piece.shape[1])  25 us
    dot_general x1, matrix products, shards(): jnp.einsum('ecf,efg->ecg', picked, expert_weight, preferred_element_type=...  21.3 us
    dot_general x4, matrix products, attend(): jnp.einsum('hqk,khd->qhd', weights, value_heads, preferred_element_type=j...  9.25 us
    unnamed x42, local copies, waits for them, and re-layouts  4.49 us
    all_to_all x1, starting transfers between devices, shards(): lax.all_to_all(activated, 'expert', split_axis=3, concat_axis=0, tiled=True)  4.09 us
    broadcast_in_dim x1, local copies, waits for them, and re-layouts, shards(): activated = jax.nn.silu(summed).astype(jnp.bfloat16)[None]  3.76 us
  transfers between devices with their start and end apart: 4, of which 4 were waited for; matrix products, arithmetic and copies ran while one was open for 5% of the time, Pallas kernels for 0%

profile of v1, /device:TPU:0, one launch (start us, length us, event | category | flops | bytes accessed | tf_op | source)
XLA Modules:
  0.0 171.1 jit_solution(16947013611806287427)
XLA Ops:
  0.7 0.8 fusion.53
  1.7 2.0 %fusion.57 = (bf16[128,1024]{1,0:T(8,128)(2,1)}, bf16[128,1024]{1,0:T(8,128)(2,1)S(1)}, bf16[128,1024]{1,0:T(8,128)(2,1)S(1)}, bf16[128,1024]{1,0:T(8,128)(2,1)S(1)}) fusion(bf16[512,1024]{1,0:T(8,128)(2,1)} %param.8), kind=kLoop, calls=%fused_computation.103 | loop fusion | bytes 2097152 | tf_op jit(solution)/shard_map/slice | solution.py:88
  4.4 1.6 multiply_select_fusion.2
  8.9 1.3 copy.115
  10.2 1.2 copy.95
  11.3 4.2 %convolution_convert_fusion.2 = bf16[8,128,128]{1,2,0:T(8,128)(2,1)S(1)} fusion(bf16[384,8,128]{0,2,1:T(8,128)(2,1)} %bitcast.113, f32[8,128]{1,0:T(8,128)S(1)} %fusion.64, f32[8,128,384]{2,1,0:T(8,128)} %multiply_select_fusion.2), kind=kOutput, calls=%fused_computation.34 | convolution fusion | flops 101975424 | bytes 2625536 | tf_op jit(solution)/shard_map/hqk,khd->qhd/dot_general | solution.py:41
  15.9 1.9 %convolution_convert_fusion.3 = bf16[8,128,128]{1,2,0:T(8,128)(2,1)S(1)} fusion(bf16[256,8,128]{0,2,1:T(8,128)(2,1)S(1)} %bitcast.114, f32[8,128]{1,0:T(8,128)S(1)} %fusion.65, f32[8,128,256]{2,1,0:T(8,128)S(1)} %fusion.19), kind=kOutput, calls=%fused_computation.35 | convolution fusion | flops 68027648 | bytes 1839104 | tf_op jit(solution)/shard_map/hqk,khd->qhd/dot_general | solution.py:41
  19.1 1.0 convolution_convert_fusion.1
  20.1 1.2 copy.100
  21.6 2.3 %fusion.61 = (f32[8,128]{1,0:T(8,128)S(1)}, f32[8,128,512]{2,1,0:T(8,128)}) fusion(pred[128,512]{1,0:T(8,128)(4,1)S(1)} %fusion.32, bf16[128,8,128]{0,2,1:T(8,128)(2,1)S(1)} %bitcast.115, bf16[512,1024]{1,0:T(8,128)(2,1)S(1)} %copy-done.7), kind=kOutput, calls=%fused_computation.107 | convolution fusion | flops 136315392 | bytes 3477504 | tf_op jit(solution)/shard_map/sub | solution.py:40
  23.9 2.1 %convolution_convert_fusion = bf16[8,128,128]{1,2,0:T(8,128)(2,1)S(1)} fusion(bf16[512,8,128]{0,2,1:T(8,128)(2,1)S(1)} %bitcast.108, f32[8,128,512]{2,1,0:T(8,128)} %get-tuple-element.26, f32[8,128]{1,0:T(8,128)S(1)} %get-tuple-element.25), kind=kOutput, calls=%fused_computation.32 | convolution fusion | flops 135397376 | bytes 3411968 | tf_op jit(solution)/shard_map/hqk,khd->qhd/dot_general | solution.py:41
  28.0 14.0 %collective-permute-done = bf16[512,1024]{1,0:T(8,128)(2,1)S(1)} collective-permute-done((bf16[512,1024]{1,0:T(8,128)(2,1)S(1)}, bf16[512,1024]{1,0:T(8,128)(2,1)S(1)}, u32[]{:S(2)}, u32[]{:S(2)}) %collective-permute-start) | collective-permute-done | bytes 1048608 | tf_op jit(solution)/shard_map/ppermute | solution.py:64
  42.3 14.0 %collective-permute-done.1 = bf16[512,1024]{1,0:T(8,128)(2,1)S(1)} collective-permute-done((bf16[512,1024]{1,0:T(8,128)(2,1)S(1)}, bf16[512,1024]{1,0:T(8,128)(2,1)S(1)}, u32[]{:S(2)}, u32[]{:S(2)}) %collective-permute-start.1) | collective-permute-done | bytes 1048608 | tf_op jit(solution)/shard_map/ppermute | solution.py:64
  56.2 2.0 %fusion.7 = pred[16,384]{1,0:T(8,128)(4,1)S(1)} fusion(s32[16,512]{1,0:T(8,128)S(1)} %convolution_convert_fusion.4, pred[16,512]{1,0:T(8,128)(4,1)S(1)} %bitcast.121), kind=kLoop, calls=%fused_computation.9 | loop fusion | flops 9431040 | bytes 47104 | tf_op jit(solution)/shard_map/reduce_or | solution.py:114
  58.3 2.8 %select_reduce_fusion = s32[16,384]{1,0:T(8,128)S(1)} fusion(s32[16,512]{1,0:T(8,128)S(1)} %convolution_convert_fusion.4, pred[16,512]{1,0:T(8,128)(4,1)S(1)} %bitcast.122), kind=kLoop, calls=%fused_computation.5 | loop fusion | flops 12576768 | bytes 65536 | tf_op jit(solution)/shard_map/reduce_sum | solution.py:115
  61.2 9.2 %collective-permute-done.2 = bf16[512,1024]{1,0:T(8,128)(2,1)S(1)} collective-permute-done((bf16[512,1024]{1,0:T(8,128)(2,1)S(1)}, bf16[512,1024]{1,0:T(8,128)(2,1)S(1)}, u32[]{:S(2)}, u32[]{:S(2)}) %collective-permute-start.2) | collective-permute-done | bytes 1048608 | tf_op jit(solution)/shard_map/ppermute | solution.py:64
  71.5 2.5 %concatenate.14 = bf16[513,4096]{1,0:T(8,128)(2,1)} pad(bf16[512,4096]{1,0:T(8,128)(2,1)S(1)} %constant_dynamic-slice_fusion.3, bf16[]{:T(256)} %constant.92.clone.1), padding=0_1x0_0 | pad | bytes 8396802 | tf_op jit(solution)/shard_map/concatenate | solution.py:124
  73.9 25.0 %gather_fusion = bf16[1536,4096]{1,0:T(8,128)(2,1)} fusion(bf16[513,4096]{1,0:T(8,128)(2,1)} %concatenate.14, s32[2048]{0:T(1024)S(1)} %pad_clamp_fusion), kind=kCustom, calls=%fused_computation | custom fusion | bytes 25171968 | tf_op jit(solution)/shard_map/gather | solution.py:125
  99.0 21.3 %fusion.11 = bf16[1,4,384,1024]{3,2,1,0:T(8,128)(2,1)S(1)} fusion(bf16[4,384,4096]{2,1,0:T(8,128)(2,1)} %bitcast.99, bf16[4,4096,1024]{2,1,0:T(8,128)(2,1)} %param.15), kind=kOutput, calls=%fused_computation.15 | convolution fusion | flops 12892766208 | bytes 49283072 | tf_op jit(solution)/shard_map/ecf,efg->ecg/dot_general | solution.py:126
  120.3 3.8 %copy.104 = bf16[1,4,384,1024]{2,1,0,3:T(4,128)(2,1)} copy(bf16[1,4,384,1024]{3,2,1,0:T(8,128)(2,1)S(1)} %fusion.11) | data formatting | bytes 6291456 | tf_op jit(solution)/shard_map/broadcast_in_dim | solution.py:127
  124.1 4.1 %all-to-all-start = ((bf16[1,4,384,1024]{2,1,0,3:T(4,128)(2,1)}), bf16[1,4,384,1024]{2,1,0,3:T(4,128)(2,1)S(1)}, u32[]{:S(2)}, u32[]{:S(2)}) async-start(bf16[1,4,384,1024]{2,1,0,3:T(4,128)(2,1)} %copy.104), calls=%async_computation | async-start | bytes 6291456 | tf_op jit(solution)/shard_map/all_to_all | solution.py:128
  138.1 26.6 %all-to-all-done = bf16[1,4,384,1024]{2,1,0,3:T(4,128)(2,1)S(1)} async-done(((bf16[1,4,384,1024]{2,1,0,3:T(4,128)(2,1)}), bf16[1,4,384,1024]{2,1,0,3:T(4,128)(2,1)S(1)}, u32[]{:S(2)}, u32[]{:S(2)}) %all-to-all-start) | async-done | bytes 3145760 | tf_op jit(solution)/shard_map/all_to_all | solution.py:128
  165.3 3.8 %fusion.8 = bf16[512,256]{0,1:T(8,128)(2,1)S(1)} fusion(f32[512,16]{0,1:T(8,128)S(1)} %select_reduce_fusion.1, bf16[16,384,256]{1,2,0:T(8,128)(2,1)S(1)} %bitcast.101, s32[16,512]{1,0:T(8,128)S(1)} %convolution_convert_fusion.4, pred[16,512]{1,0:T(8,128)(4,1)S(1)} %bitcast.123), kind=kOutput, calls=%fused_computation.11 | convolution fusion | flops 1620967424 | bytes 3481600 | tf_op jit(solution)/shard_map/ect,ecg->teg/dot_general | solution.py:130
  169.1 0.8 copy.106
  (102 shorter events, 12.3 us)
Async XLA Ops:
  0.6 3.3 %slice-start.3 = ((bf16[512,1024]{1,0:T(8,128)(2,1)}), bf16[384,1024]{1,0:T(8,128)(2,1)S(1)}, s32[]{:S(2)}) async-start(bf16[512,1024]{1,0:T(8,128)(2,1)} %param.9), calls=%async_computation.4 | async-start | bytes 1572864 | tf_op jit(solution)/shard_map/slice | solution.py:89
  4.4 2.5 %slice-start.4 = ((bf16[512,1024]{1,0:T(8,128)(2,1)}), bf16[256,1024]{1,0:T(8,128)(2,1)S(1)}, s32[]{:S(2)}) async-start(bf16[512,1024]{1,0:T(8,128)(2,1)} %param.9), calls=%async_computation.5 | async-start | bytes 1048576 | tf_op jit(solution)/shard_map/slice | solution.py:89
  7.6 1.2 copy-start
  8.3 1.9 %slice-start = ((bf16[512,1024]{1,0:T(8,128)(2,1)}), bf16[384,1024]{1,0:T(8,128)(2,1)S(1)}, s32[]{:S(2)}) async-start(bf16[512,1024]{1,0:T(8,128)(2,1)} %param.10), calls=%async_computation.1 | async-start | bytes 1572864 | tf_op jit(solution)/shard_map/slice | solution.py:90
  11.3 4.3 %slice-start.1 = ((bf16[512,1024]{1,0:T(8,128)(2,1)}), bf16[256,1024]{1,0:T(8,128)(2,1)S(1)}, s32[]{:S(2)}) async-start(bf16[512,1024]{1,0:T(8,128)(2,1)} %param.10), calls=%async_computation.2 | async-start | bytes 1048576 | tf_op jit(solution)/shard_map/slice | solution.py:90
  15.7 2.4 %copy-start.10 = (bf16[128,1024]{1,0:T(8,128)(2,1)S(1)}, bf16[128,1024]{1,0:T(8,128)(2,1)}, u32[]{:S(2)}) copy-start(bf16[128,1024]{1,0:T(8,128)(2,1)} %get-tuple-element.9) | copy-start | bytes 786436
  15.9 2.4 %slice-start.5 = ((bf16[512,1024]{1,0:T(8,128)(2,1)}), bf16[128,1024]{1,0:T(8,128)(2,1)S(1)}, s32[]{:S(2)}) async-start(bf16[512,1024]{1,0:T(8,128)(2,1)} %param.9), calls=%async_computation.6 | async-start | bytes 524288 | tf_op jit(solution)/shard_map/slice | solution.py:89
  15.9 3.0 %slice-start.2 = ((bf16[512,1024]{1,0:T(8,128)(2,1)}), bf16[128,1024]{1,0:T(8,128)(2,1)S(1)}, s32[]{:S(2)}) async-start(bf16[512,1024]{1,0:T(8,128)(2,1)} %param.10), calls=%async_computation.3 | async-start | bytes 524288 | tf_op jit(solution)/shard_map/slice | solution.py:90
  18.0 8.2 %copy-start.1 = (bf16[128,1024]{1,0:T(8,128)(2,1)}, bf16[128,1024]{1,0:T(8,128)(2,1)S(1)}, u32[]{:S(2)}) copy-start(bf16[128,1024]{1,0:T(8,128)(2,1)S(1)} %copy.101) | copy-start | bytes 786436
  18.3 3.3 %copy-start.7 = (bf16[512,1024]{1,0:T(8,128)(2,1)S(1)}, bf16[512,1024]{1,0:T(8,128)(2,1)}, u32[]{:S(2)}) copy-start(bf16[512,1024]{1,0:T(8,128)(2,1)} %param.9) | copy-start | bytes 3145732
  20.1 3.9 %copy-start.9 = (bf16[512,1024]{0,1:T(8,128)(2,1)S(1)}, bf16[512,1024]{0,1:T(8,128)(2,1)}, u32[]{:S(2)}) copy-start(bf16[512,1024]{0,1:T(8,128)(2,1)} %copy.115) | copy-start | bytes 3145732
  21.3 5.0 %copy-start.3 = (bf16[128,1024]{1,0:T(8,128)(2,1)}, bf16[128,1024]{1,0:T(8,128)(2,1)S(1)}, u32[]{:S(2)}) copy-start(bf16[128,1024]{1,0:T(8,128)(2,1)S(1)} %copy.100) | copy-start | bytes 786436
  23.9 18.1 %copy-start.11 = (s32[512,8]{0,1:T(8,128)S(1)}, s32[512,8]{0,1:T(8,128)}, u32[]{:S(2)}) copy-start(s32[512,8]{0,1:T(8,128)} %param.13) | copy-start | bytes 49156
  26.3 0.7 copy-start.5
  27.0 1.0 copy-start.8
  27.0 14.9 %collective-permute-start = (bf16[512,1024]{1,0:T(8,128)(2,1)S(1)}, bf16[512,1024]{1,0:T(8,128)(2,1)S(1)}, u32[]{:S(2)}, u32[]{:S(2)}) collective-permute-start(bf16[512,1024]{1,0:T(8,128)(2,1)S(1)} %pad_maximum_fusion), channel_id=1, source_target_pairs={{0,1},{1,2},{2,3},{3,0},{4,5},{5,6},{6,7},{7,4},{8,9},{9,10},{10,1... | collective-permute-start | bytes 3145736 | tf_op jit(solution)/shard_map/ppermute | solution.py:64
  42.0 14.2 %collective-permute-start.1 = (bf16[512,1024]{1,0:T(8,128)(2,1)S(1)}, bf16[512,1024]{1,0:T(8,128)(2,1)S(1)}, u32[]{:S(2)}, u32[]{:S(2)}) collective-permute-start(bf16[512,1024]{1,0:T(8,128)(2,1)S(1)} %collective-permute-done), channel_id=1, source_target_pairs={{0,1},{1,2},{2,3},{3,0},{4,5},{5,6},{6,7},{7,4},{8,9},{9,10},{10,1... | collective-permute-start | bytes 3145736 | tf_op jit(solution)/shard_map/ppermute | solution.py:64
  56.2 14.2 %collective-permute-start.2 = (bf16[512,1024]{1,0:T(8,128)(2,1)S(1)}, bf16[512,1024]{1,0:T(8,128)(2,1)S(1)}, u32[]{:S(2)}, u32[]{:S(2)}) collective-permute-start(bf16[512,1024]{1,0:T(8,128)(2,1)S(1)} %collective-permute-done.1), channel_id=1, source_target_pairs={{0,1},{1,2},{2,3},{3,0},{4,5},{5,6},{6,7},{7,4},{8,9},{9,10},{10,1... | collective-permute-start | bytes 3145736 | tf_op jit(solution)/shard_map/ppermute | solution.py:64
  61.2 9.5 %copy-start.2 = (bf16[128,1024]{1,0:T(8,128)(2,1)S(1)}, bf16[128,1024]{1,0:T(8,128)(2,1)}, u32[]{:S(2)}) copy-start(bf16[128,1024]{1,0:T(8,128)(2,1)} %copy-done.1) | copy-start | bytes 786436
  61.2 9.5 %copy-start.4 = (bf16[128,1024]{1,0:T(8,128)(2,1)S(1)}, bf16[128,1024]{1,0:T(8,128)(2,1)}, u32[]{:S(2)}) copy-start(bf16[128,1024]{1,0:T(8,128)(2,1)} %copy-done.3) | copy-start | bytes 786436
  61.2 9.5 %copy-start.6 = (bf16[128,1024]{1,0:T(8,128)(2,1)S(1)}, bf16[128,1024]{1,0:T(8,128)(2,1)}, u32[]{:S(2)}) copy-start(bf16[128,1024]{1,0:T(8,128)(2,1)} %copy-done.5) | copy-start | bytes 786436
  124.1 4.1 %copy-start.13 = (s32[8,2]{0,1:T(2,128)S(1)}, s32[8,2]{0,1:T(2,128)}, u32[]{:S(2)}) copy-start(s32[8,2]{0,1:T(2,128)} %param.12) | copy-start | bytes 196
  124.1 14.0 %copy-start.12 = (f32[512,8]{0,1:T(8,128)S(1)}, f32[512,8]{0,1:T(8,128)}, u32[]{:S(2)}) copy-start(f32[512,8]{0,1:T(8,128)} %param.14) | copy-start | bytes 49156
  124.1 40.7 %all-to-all-start = ((bf16[1,4,384,1024]{2,1,0,3:T(4,128)(2,1)}), bf16[1,4,384,1024]{2,1,0,3:T(4,128)(2,1)S(1)}, u32[]{:S(2)}, u32[]{:S(2)}) async-start(bf16[1,4,384,1024]{2,1,0,3:T(4,128)(2,1)} %copy.104), calls=%async_computation | async-start | bytes 6291456 | tf_op jit(solution)/shard_map/all_to_all | solution.py:128
